TPU v7x, 32 devices: a whole 2x2x4 slice. The times are simulated.
32 devices in a mesh: grp: 2 (over y), gx: 4 (over z), gy: 2 (over x), gz: 2 (over core).
Axes of the slice: x: 2, y: 2, z: 4, core: 2. Of those that a mesh axis runs over, the one named last changes fastest.
Arguments:
- alignment_token_ids: int32 [128, 128], P(('grp', 'gx'), ('gy', 'gz')), parts along dimension 0, may hold values from 0 to 22
- homolog_profile: bfloat16 [128, 128, 256], P(('grp', 'gx'), ('gy', 'gz')), parts along dimension 0, may hold values from -6 to 6
- alignment_mask: int32 [128, 128], P(('grp', 'gx'), ('gy', 'gz')), parts along dimension 0, may hold values 0 or 1
- pair_features: bfloat16 [256, 128, 128], P(('grp', 'gy', 'gz'), 'gx'), parts along dimension 0, may hold values from -4 to 6
- symbol_lookup_weights: bfloat16 [23, 256], replicated, may hold values from -6 to 6
- asking_weights: bfloat16 [256, 256], replicated, may hold values from -0.375 to 0.375
- lookup_weights: bfloat16 [256, 256], replicated, may hold values from -0.375 to 0.375
- content_weights: bfloat16 [256, 256], replicated, may hold values from -0.375 to 0.375
- sigmoid_switch_weights: bfloat16 [256, 256], replicated, may hold values from -0.375 to 0.375
- resulting_weights: bfloat16 [256, 256], replicated, may hold values from -0.75 to 0.75
- pair_bias_matrix: float32 [128, 8], replicated, may hold values from -0.9 to 48
- first_factor_weights: bfloat16 [256, 32], replicated, may hold values from -0.375 to 0.375
- second_factor_weights: bfloat16 [256, 32], replicated, may hold values from -0.375 to 0.375
- outer_mixing_weight: bfloat16 [1024, 128], replicated, may hold values from -1 to 1
- widening_weight: bfloat16 [128, 512], replicated, may hold values from -0.5 to 0.5
- narrowing_weight: bfloat16 [512, 128], replicated, may hold values from -0.375 to 0.375
Outputs:
- profile_refreshed: bfloat16 [128, 128, 256], P(('grp', 'gx'), ('gy', 'gz')), parts along dimension 0
- pair_output: bfloat16 [256, 128, 128], P(('grp', 'gy', 'gz'), 'gx'), parts along dimension 0
There are 2 independent parts, one for each index of `grp`. A program takes and returns all parts, laid end to end along the dimension named above; an argument that names none is the same for every part. Nothing has to cross between parts.
All inputs are finite; a program needn't handle non-finite values. No bound on the sum of `alignment_mask` on one device may be relied on, other than what follows from the above.
Results may differ from a plain program's by a relative error of at most 0.013.
Values may be sent and summed in bfloat16 or wider, within the bound.
A program may use at most 64 MiB of HBM per device.

v0:
```python
import jax
import jax.numpy as jnp
from jax import lax
from jax.sharding import PartitionSpec as P


def standardize_lastaxis(values):
    average = jnp.mean(values, axis=-1, keepdims=True)
    centred = values - average
    return centred * lax.rsqrt(jnp.mean(centred * centred, axis=-1, keepdims=True) + 1e-05)


def attend(state, queries, key_piece, value_piece, valid_piece, bias_rows):
    sequence_total, residue_total, feature_vectors = queries.shape
    piece_len = key_piece.shape[1]
    head_count = bias_rows.shape[1]
    head_size = feature_vectors // head_count
    running_max, running_sum, weighted = state
    scores = jnp.einsum(
        "sihd,sjhd->sihj",
        queries.reshape(sequence_total, residue_total, head_count, head_size),
        key_piece.reshape(sequence_total, piece_len, head_count, head_size),
        preferred_element_type=jnp.float32,
    ) * head_size ** (-0.5)
    scores = (
        scores
        + bias_rows[None]
        + ((valid_piece.astype(jnp.float32) - 1.0) * 1000000000.0)[:, None, None, :]
    )
    new_max = jnp.max(scores, axis=-1)
    rescale = jnp.exp(running_max - new_max)
    exp_scores = jnp.exp(scores - new_max[:, :, :, None])
    new_sum = running_sum * rescale + jnp.sum(exp_scores, axis=-1)
    accumulated = jnp.einsum(
        "sihj,sjhd->sihd",
        exp_scores.astype(jnp.bfloat16),
        value_piece.reshape(sequence_total, piece_len, head_count, head_size),
        preferred_element_type=jnp.float32,
    )
    new_weighted = (
        weighted.reshape(sequence_total, residue_total, head_count, head_size)
        * rescale[:, :, :, None]
        + accumulated
    )
    return (new_max, new_sum, new_weighted.reshape(sequence_total, residue_total, feature_vectors))


def local(
    alignment_token_ids,
    homolog_profile,
    alignment_mask,
    pair_features,
    symbol_lookup_weights,
    asking_weights,
    lookup_weights,
    content_weights,
    sigmoid_switch_weights,
    resulting_weights,
    pair_bias_matrix,
    first_factor_weights,
    second_factor_weights,
    outer_mixing_weight,
    widening_weight,
    narrowing_weight,
):
    sequence_total, residue_total, feature_vectors = homolog_profile.shape
    head_count = pair_bias_matrix.shape[1]
    side_width = first_factor_weights.shape[1]
    pair_width = pair_features.shape[2]
    class_labels = jnp.arange(symbol_lookup_weights.shape[0], dtype=jnp.int32)
    indicator_encoding = (alignment_token_ids[:, :, None] == class_labels).astype(jnp.bfloat16)
    profile_arriving = homolog_profile.astype(jnp.float32) + jnp.einsum(
        "srv,vc->src", indicator_encoding, symbol_lookup_weights, preferred_element_type=jnp.float32
    )
    standardized_profile = standardize_lastaxis(profile_arriving).astype(jnp.bfloat16)
    flat_rows = standardized_profile.reshape(sequence_total * residue_total, feature_vectors)

    def project(row_block, weight, row_total):
        return (
            jnp.dot(row_block, weight, preferred_element_type=jnp.float32)
            .astype(jnp.bfloat16)
            .reshape(sequence_total, row_total, feature_vectors)
        )

    queries = project(flat_rows, asking_weights, residue_total)
    sigmoid_switch = jax.nn.sigmoid(
        jnp.dot(flat_rows, sigmoid_switch_weights, preferred_element_type=jnp.float32)
    ).reshape(sequence_total, residue_total, feature_vectors)
    validity_mask = alignment_mask.astype(jnp.bfloat16)
    pair_normed = standardize_lastaxis(pair_features.astype(jnp.float32))
    bias_local = jnp.einsum(
        "ijc,ch->ihj", pair_normed, pair_bias_matrix, precision=lax.Precision.HIGHEST
    )
    bias_rows = lax.all_gather(bias_local, "gx", axis=2, tiled=True)
    start_state = (
        jnp.full((sequence_total, residue_total, head_count), -jnp.inf, jnp.float32),
        jnp.zeros((sequence_total, residue_total, head_count), jnp.float32),
        jnp.zeros((sequence_total, residue_total, feature_vectors), jnp.float32),
    )
    keys_local = project(flat_rows, lookup_weights, residue_total)
    values_local = project(flat_rows, content_weights, residue_total)
    final_state = attend(
        start_state,
        queries,
        lax.all_gather(keys_local, ("gy", "gz"), axis=1, tiled=True),
        lax.all_gather(values_local, ("gy", "gz"), axis=1, tiled=True),
        lax.all_gather(validity_mask, ("gy", "gz"), axis=1, tiled=True),
        bias_rows,
    )
    softmax_combined = (
        final_state[2].reshape(
            sequence_total, residue_total, head_count, feature_vectors // head_count
        )
        / final_state[1][:, :, :, None]
    )
    switched_result = (
        sigmoid_switch * softmax_combined.reshape(sequence_total, residue_total, feature_vectors)
    ).astype(jnp.bfloat16)
    attention_projector = jnp.dot(
        switched_result.reshape(sequence_total * residue_total, feature_vectors),
        resulting_weights,
        preferred_element_type=jnp.float32,
    )
    profile_refreshed = (
        profile_arriving
        + attention_projector.reshape(sequence_total, residue_total, feature_vectors)
    ).astype(jnp.bfloat16)
    averaged_products = (
        standardize_lastaxis(profile_refreshed.astype(jnp.float32))
        .astype(jnp.bfloat16)
        .reshape(sequence_total * residue_total, feature_vectors)
    )
    mask_floating = alignment_mask.astype(jnp.float32)[:, :, None]
    left_side = (
        (
            jnp.dot(
                averaged_products, first_factor_weights, preferred_element_type=jnp.float32
            ).reshape(sequence_total, residue_total, side_width)
            * mask_floating
        )
        .astype(jnp.bfloat16)
        .reshape(sequence_total, residue_total * side_width)
    )
    right_side = (
        (
            jnp.dot(
                averaged_products, second_factor_weights, preferred_element_type=jnp.float32
            ).reshape(sequence_total, residue_total, side_width)
            * mask_floating
        )
        .astype(jnp.bfloat16)
        .reshape(sequence_total, residue_total * side_width)
    )
    left_all, mask_rows = (
        lax.all_gather(left_side, "gx", axis=0, tiled=True),
        lax.all_gather(validity_mask, "gx", axis=0, tiled=True),
    )
    right_wide, mask_wide = (
        lax.all_gather(right_side, ("gy", "gz"), axis=1, tiled=True),
        lax.all_gather(validity_mask, ("gy", "gz"), axis=1, tiled=True),
    )
    right_cols, mask_cols = (
        lax.all_to_all(right_wide, "gx", split_axis=1, concat_axis=0, tiled=True),
        lax.all_to_all(mask_wide, "gx", split_axis=1, concat_axis=0, tiled=True),
    )
    pair_count = jnp.einsum("si,sj->ij", mask_rows, mask_cols, preferred_element_type=jnp.float32)
    panel_rows = 16

    def outer_panel(panel_index):
        left_rows = lax.dynamic_slice_in_dim(
            left_all, panel_index * (panel_rows * side_width), panel_rows * side_width, 1
        )
        outer_block = jnp.einsum(
            "sa,sb->ab", left_rows, right_cols, preferred_element_type=jnp.float32
        ).astype(jnp.bfloat16)
        outer_block = (
            outer_block.reshape(panel_rows, side_width, residue_total, side_width)
            .transpose(0, 2, 1, 3)
            .reshape(panel_rows * residue_total, side_width * side_width)
        )
        return jnp.dot(
            outer_block, outer_mixing_weight, preferred_element_type=jnp.float32
        ).reshape(panel_rows, residue_total, pair_width)

    mixed_pair = lax.map(
        outer_panel, jnp.arange(residue_total // panel_rows, dtype=jnp.int32)
    ).reshape(residue_total, residue_total, pair_width)
    pair_mid = pair_features.astype(jnp.float32) + mixed_pair / (pair_count[:, :, None] + 1.0)
    trans_rows = (
        standardize_lastaxis(pair_mid)
        .astype(jnp.bfloat16)
        .reshape(residue_total * residue_total, pair_width)
    )
    expanded = jax.nn.relu(
        jnp.dot(trans_rows, widening_weight, preferred_element_type=jnp.float32)
    ).astype(jnp.bfloat16)
    pair_output = (
        pair_mid
        + jnp.dot(expanded, narrowing_weight, preferred_element_type=jnp.float32).reshape(
            residue_total, residue_total, pair_width
        )
    ).astype(jnp.bfloat16)
    return (profile_refreshed, pair_output)


def solution(mesh):
    in_specs = (
        P(("grp", "gx"), ("gy", "gz")),
        P(("grp", "gx"), ("gy", "gz"), None),
        P(("grp", "gx"), ("gy", "gz")),
        P(("grp", "gy", "gz"), "gx", None),
        P(),
        P(),
        P(),
        P(),
        P(),
        P(),
        P(),
        P(),
        P(),
        P(),
        P(),
        P(),
    )
    out_specs = (P(("grp", "gx"), ("gy", "gz"), None), P(("grp", "gy", "gz"), "gx", None))
    return jax.shard_map(local, mesh=mesh, in_specs=in_specs, out_specs=out_specs, check_vma=False)
```

profile of v0, /device:TPU:0, one launch (start us, length us, event | category | flops | bytes accessed | tf_op | source)
XLA Modules:
  0.0 149.4 jit_solution(12472776725563297926)
XLA Ops:
  7.2 0.0 copy-start
  7.2 0.0 all-gather.4.cloned.1.call-start
  7.3 1.5 fusion.43
  8.8 0.3 multiply_reduce_fusion.1
  9.0 0.2 multiply_convert_fusion.1
  9.3 0.9 convolution_convert_fusion.3
  10.2 0.0 all-gather.4.cloned.1.call-update
  10.2 0.6 fusion.42
  10.8 6.2 %all-gather = bf16[4,32,16]{1,2,0:T(8,128)(2,1)S(1)} all-gather(bf16[1,32,16]{1,2,0:T(8,128)(2,1)S(1)} %bitcast.123), channel_id=1, replica_groups=mesh['grp'=2,'gx'=4,'gy'=2,'gz'=2] {'gy','gz'}, dimensions={0}, use_global_device_ids=true | all-gather | bytes 5120 | tf_op jit(solution)/shard_map/all_gather | solution.py:107
  17.1 0.1 reshape.151
  17.2 0.1 all_to_all.32
  17.2 0.7 reshape.161
  17.9 5.3 %all-to-all-start.1 = ((bf16[4,2,256]{2,1,0:T(2,128)(2,1)}), bf16[4,2,256]{2,1,0:T(2,128)(2,1)S(1)}, u32[]{:S(2)}, u32[]{:S(2)}) async-start(bf16[4,2,256]{2,1,0:T(2,128)(2,1)} %reshape.161), calls=%async_computation.1 | async-start | bytes 8192 | tf_op jit(solution)/shard_map/all_to_all | solution.py:164
  23.3 0.9 convolution_convert_fusion.1
  24.2 0.0 all-gather.6.cloned.1.call-update
  24.2 0.2 convert_reduce_fusion
  24.4 0.4 fusion.25
  24.9 2.2 %convolution_bitcast_fusion.1 = f32[32,8,32]{2,1,0:T(8,128)S(1)} fusion(bf16[32,32,128]{2,1,0:T(8,128)(2,1)S(1)} %copy-done.1, f32[32,32]{1,0:T(8,128)S(1)} %add_rsqrt_fusion.1, f32[32,32]{1,0:T(8,128)S(1)} %broadcast_multiply_fusion.1, f32[128,8]{0,1:T(8,128)S(1)} %copy-done.15), kind=kOutput, calls=%fused_computation.31 | convolution fusion | flops 12976128 | bytes 307200 | tf_op jit(solution)/shard_map/ijc,ch->ihj/dot_general | solution.py:91
  27.1 0.1 copy.37
  27.2 0.2 convolution_convert_fusion.2
  27.5 16.1 %all_gather.23 = f32[32,8,128]{0,1,2:T(8,128)S(1)} all-gather(f32[32,8,32]{0,1,2:T(8,128)S(1)} %copy.37), channel_id=1, replica_groups=mesh['grp'=2,'gx'=4,'gy'=2,'gz'=2] {'gx'}, dimensions={2}, use_global_device_ids=true | all-gather | bytes 163840 | tf_op jit(solution)/shard_map/all_gather | solution.py:94
  43.6 1.4 reshape_reshape.3
  45.0 0.2 copy.38
  45.2 13.5 %all_gather.28 = bf16[64,32]{1,0:T(8,128)(2,1)S(1)} all-gather(bf16[16,32]{1,0:T(8,128)(2,1)S(1)} %get-tuple-element.50), channel_id=1, replica_groups=mesh['grp'=2,'gx'=4,'gy'=2,'gz'=2] {'gx'}, dimensions={0}, use_global_device_ids=true | all-gather | bytes 5120 | tf_op jit(solution)/shard_map/all_gather | solution.py:156
  58.7 0.1 reshape.162
  58.8 0.2 convolution_add_fusion.2
  59.0 2.3 %copy.35 = bf16[16,128,256]{1,2,0:T(8,128)(2,1)} copy(bf16[16,128,256]{2,1,0:T(8,128)(2,1)} %all-gather.4.cloned.1.call-done) | data formatting | bytes 2097152 | tf_op jit(solution)/shard_map/all_gather | solution.py:105
  61.3 2.3 %fusion.44 = (f32[16,32,8]{1,2,0:T(8,128)S(1)}, f32[16,32,8,128]{3,1,2,0:T(8,128)S(1)}) fusion(f32[16,128]{1,0:T(8,128)S(1)} %add_multiply_fusion, f32[32,8,128]{2,0,1:T(8,128)S(1)} %copy.38, bf16[16,128,8,32]{1,3,2,0:T(8,128)(2,1)} %bitcast.113, bf16[16,32,8,32]{3,2,1,0:T(8,128)(2,1)} %reshape_reshape.3), kind=kOutput, calls=%fused_computation.79 | convolution fusion | flops 35647488 | bytes 3563520 | tf_op jit(solution)/shard_map/sihd,sjhd->sihj/dot_general | solution.py:19
  63.6 1.3 fusion.6
  64.9 0.0 all-gather.6.cloned.1.call-done
  65.0 2.3 %copy.40 = bf16[16,128,256]{1,2,0:T(8,128)(2,1)} copy(bf16[16,128,256]{2,1,0:T(8,128)(2,1)} %all-gather.6.cloned.1.call-done) | data formatting | bytes 2097152 | tf_op jit(solution)/shard_map/all_gather | solution.py:106
  67.2 3.3 %fusion.4 = f32[16,32,8,32]{1,3,2,0:T(8,128)} fusion(bf16[16,128,8,32]{1,3,2,0:T(8,128)(2,1)} %bitcast.114, f32[16,32,8,128]{3,1,2,0:T(8,128)S(1)} %get-tuple-element.54, f32[16,32,8]{1,2,0:T(8,128)S(1)} %get-tuple-element.48, f32[16,32,8]{1,2,0:T(8,128)S(1)} %get-tuple-element.53, f32[16,32,8]{1,2,0:T(8,128)S(1)} %get-tuple-element.47), kind=kOutput, calls=%fused_computation.7 | convolution fusion | flops 34865152 | bytes 3719168 | tf_op jit(solution)/shard_map/sihj,sjhd->sihd/dot_general | solution.py:34
  70.6 2.0 %copy.41 = f32[16,32,8,32]{3,2,1,0:T(8,128)S(1)} copy(f32[16,32,8,32]{1,3,2,0:T(8,128)} %fusion.4) | data formatting | bytes 1048576 | tf_op jit(solution)/shard_map/div | solution.py:111
  72.6 1.4 reshape.144
  74.0 1.4 fusion.13
  75.4 0.3 convert_reduce_fusion.1
  75.7 0.3 fusion.27
  76.0 0.3 fusion.16
  76.3 0.2 reshape.146
  76.5 5.4 %all_gather.27 = bf16[16,4096]{1,0:T(8,128)(2,1)S(1)} all-gather(bf16[16,1024]{1,0:T(8,128)(2,1)S(1)} %reshape.146), channel_id=1, replica_groups=mesh['grp'=2,'gx'=4,'gy'=2,'gz'=2] {'gy','gz'}, dimensions={1}, use_global_device_ids=true | all-gather | bytes 163840 | tf_op jit(solution)/shard_map/all_gather | solution.py:159
  81.9 0.7 copy.51
  82.6 5.1 %all-to-all-start = ((bf16[16,4,1024]{2,0,1:T(8,128)(2,1)}), bf16[16,4,1024]{2,0,1:T(8,128)(2,1)S(1)}, u32[]{:S(2)}, u32[]{:S(2)}) async-start(bf16[16,4,1024]{2,0,1:T(8,128)(2,1)} %bitcast.93), calls=%async_computation | async-start | bytes 262144 | tf_op jit(solution)/shard_map/all_to_all | solution.py:163
  87.7 0.3 fusion.15
  88.0 0.2 reshape.145
  88.2 14.1 %all_gather.26 = bf16[64,1024]{1,0:T(8,128)(2,1)S(1)} all-gather(bf16[16,1024]{1,0:T(8,128)(2,1)S(1)} %reshape.145), channel_id=1, replica_groups=mesh['grp'=2,'gx'=4,'gy'=2,'gz'=2] {'gx'}, dimensions={0}, use_global_device_ids=true | all-gather | bytes 163840 | tf_op jit(solution)/shard_map/all_gather | solution.py:155
  102.3 37.2 %while.10 = (s32[]{:T(128)}, f32[2,16,32,128]{3,2,1,0:T(8,128)S(1)}, s32[2]{0:T(128)S(1)}, bf16[64,1024]{1,0:T(8,128)(2,1)S(1)}, bf16[64,1024]{1,0:T(8,128)(2,1)...) while((s32[]{:T(128)}, f32[2,16,32,128]{3,2,1,0:T(8,128)S(1)}, ...), condition=%wide.region_9.10_spmd, body=%wide.region_8.9_spmd.sunk | while | flops 201850880 | bytes 9109671 | solution.py:185
  102.4 0.6 dynamic_slice.12
  103.6 0.5 convolution_convert_fusion.5
  104.1 4.4 %reshape.165 = bf16[16,32,32,32]{3,2,1,0:T(8,128)(2,1)} reshape(bf16[512,1024]{1,0:T(8,128)(2,1)S(1)} %convolution_convert_fusion.5) | data formatting | bytes 2097152 | tf_op jit(solution)/shard_map/while/body/eval_jaxpr/reshape | solution.py:177
  108.4 5.9 %copy.54 = bf16[16,32,32,32]{3,2,1,0:T(8,128)(2,1)} copy(bf16[16,32,32,32]{3,1,2,0:T(8,128)(2,1)} %bitcast.107) | data formatting | bytes 2097152 | tf_op jit(solution)/shard_map/while/body/eval_jaxpr/transpose | solution.py:178
  114.3 6.2 %reshape.166 = bf16[16,32,1024]{2,1,0:T(8,128)(2,1)S(1)} reshape(bf16[16,32,32,32]{3,2,1,0:T(8,128)(2,1)} %copy.54) | data formatting | bytes 2097152 | tf_op jit(solution)/shard_map/reshape.62
  120.5 0.4 fusion.72
  121.0 0.6 dynamic_slice.12
  122.2 0.5 convolution_convert_fusion.5
  122.7 4.4 %reshape.165 = bf16[16,32,32,32]{3,2,1,0:T(8,128)(2,1)} reshape(bf16[512,1024]{1,0:T(8,128)(2,1)S(1)} %convolution_convert_fusion.5) | data formatting | bytes 2097152 | tf_op jit(solution)/shard_map/while/body/eval_jaxpr/reshape | solution.py:177
  127.0 5.9 %copy.54 = bf16[16,32,32,32]{3,2,1,0:T(8,128)(2,1)} copy(bf16[16,32,32,32]{3,1,2,0:T(8,128)(2,1)} %bitcast.107) | data formatting | bytes 2097152 | tf_op jit(solution)/shard_map/while/body/eval_jaxpr/transpose | solution.py:178
  133.0 6.2 %reshape.166 = bf16[16,32,1024]{2,1,0:T(8,128)(2,1)S(1)} reshape(bf16[16,32,32,32]{3,2,1,0:T(8,128)(2,1)} %copy.54) | data formatting | bytes 2097152 | tf_op jit(solution)/shard_map/reshape.62
  139.1 0.4 fusion.72
  139.6 0.2 bitcast_divide_fusion
  139.8 0.2 fusion.35
  140.1 0.4 multiply_reduce_fusion
  140.5 0.5 multiply_convert_fusion
  141.0 0.7 fusion.8
  141.6 0.9 add_convert_fusion
  (49 shorter events, 0.2 us)
Async XLA Ops:
  7.2 68.2 %copy-start = (bf16[256,256]{1,0:T(8,128)(2,1)S(1)}, bf16[256,256]{1,0:T(8,128)(2,1)}, u32[]{:S(2)}) copy-start(bf16[256,256]{1,0:T(8,128)(2,1)} %param.27) | copy-start | bytes 393220
  7.2 2.1 %copy-start.5 = (bf16[256,256]{1,0:T(8,128)(2,1)S(1)}, bf16[256,256]{1,0:T(8,128)(2,1)}, u32[]{:S(2)}) copy-start(bf16[256,256]{1,0:T(8,128)(2,1)} %param.24) | copy-start | bytes 393220
  7.2 3.0 %copy-start.8 = (s32[16,32]{1,0:T(8,128)S(1)}, s32[16,32]{1,0:T(8,128)}, u32[]{:S(2)}) copy-start(s32[16,32]{1,0:T(8,128)} %param.20) | copy-start | bytes 6148
  7.2 16.1 %copy-start.6 = (bf16[256,256]{1,0:T(8,128)(2,1)S(1)}, bf16[256,256]{1,0:T(8,128)(2,1)}, u32[]{:S(2)}) copy-start(bf16[256,256]{1,0:T(8,128)(2,1)} %param.25) | copy-start | bytes 393220
  7.2 17.0 %copy-start.1 = (bf16[32,32,128]{2,1,0:T(8,128)(2,1)S(1)}, bf16[32,32,128]{2,1,0:T(8,128)(2,1)}, u32[]{:S(2)}) copy-start(bf16[32,32,128]{2,1,0:T(8,128)(2,1)} %param.21) | copy-start | bytes 786436
  7.2 51.8 %all-gather.4.cloned.1.call-start = ((), (), s32[]{:S(2)}) async-start(), calls=%async_computation.2 | async-start | bytes 1310720 | tf_op jit(solution)/shard_map/all_gather | solution.py:105
  8.7 16.1 %copy-start.15 = (f32[128,8]{0,1:T(8,128)S(1)}, f32[128,8]{0,1:T(8,128)}, u32[]{:S(2)}) copy-start(f32[128,8]{0,1:T(8,128)} %param.28) | copy-start | bytes 12292
  9.0 18.2 %copy-start.7 = (bf16[256,256]{1,0:T(8,128)(2,1)S(1)}, bf16[256,256]{1,0:T(8,128)(2,1)}, u32[]{:S(2)}) copy-start(bf16[256,256]{1,0:T(8,128)(2,1)} %param.23) | copy-start | bytes 393220
  17.9 40.8 %all-to-all-start.1 = ((bf16[4,2,256]{2,1,0:T(2,128)(2,1)}), bf16[4,2,256]{2,1,0:T(2,128)(2,1)S(1)}, u32[]{:S(2)}, u32[]{:S(2)}) async-start(bf16[4,2,256]{2,1,0:T(2,128)(2,1)} %reshape.161), calls=%async_computation.1 | async-start | bytes 8192 | tf_op jit(solution)/shard_map/all_to_all | solution.py:164
  23.3 41.7 %all-gather.6.cloned.1.call-start = ((), (), s32[]{:S(2)}) async-start(), calls=%async_computation.3 | async-start | bytes 1310720 | tf_op jit(solution)/shard_map/all_gather | solution.py:106
  72.6 1.4 copy-start.10
  74.0 2.0 %copy-start.9 = (f32[16,32]{1,0:T(8,128)S(1)}, f32[16,32]{1,0:T(8,128)}, u32[]{:S(2)}) copy-start(f32[16,32]{1,0:T(8,128)} %get-tuple-element.49) | copy-start | bytes 6148
  74.0 2.0 %copy-start.13 = (bf16[256,32]{0,1:T(8,128)(2,1)S(1)}, bf16[256,32]{0,1:T(8,128)(2,1)}, u32[]{:S(2)}) copy-start(bf16[256,32]{0,1:T(8,128)(2,1)} %param.30) | copy-start | bytes 49156
  75.3 12.4 %copy-start.14 = (bf16[256,32]{0,1:T(8,128)(2,1)S(1)}, bf16[256,32]{0,1:T(8,128)(2,1)}, u32[]{:S(2)}) copy-start(bf16[256,32]{0,1:T(8,128)(2,1)} %param.29) | copy-start | bytes 49156
  75.3 27.0 %copy-start.2 = (bf16[1024,128]{1,0:T(8,128)(2,1)S(1)}, bf16[1024,128]{1,0:T(8,128)(2,1)}, u32[]{:S(2)}) copy-start(bf16[1024,128]{1,0:T(8,128)(2,1)} %param.31) | copy-start | bytes 786436
  75.4 27.0 %copy-start.3 = (f32[2,16,32,128]{3,2,1,0:T(8,128)S(1)}, f32[2,16,32,128]{3,2,1,0:T(8,128)}, u32[]{:S(2)}) copy-start(f32[2,16,32,128]{3,2,1,0:T(8,128)} %custom-call) | copy-start | bytes 1572868
  75.7 26.6 %copy-start.4 = (bf16[16,32,256]{2,1,0:T(8,128)(2,1)}, bf16[16,32,256]{2,1,0:T(8,128)(2,1)S(1)}, u32[]{:S(2)}) copy-start(bf16[16,32,256]{2,1,0:T(8,128)(2,1)S(1)} %get-tuple-element.56) | copy-start | bytes 786436
  82.6 19.7 %all-to-all-start = ((bf16[16,4,1024]{2,0,1:T(8,128)(2,1)}), bf16[16,4,1024]{2,0,1:T(8,128)(2,1)S(1)}, u32[]{:S(2)}, u32[]{:S(2)}) async-start(bf16[16,4,1024]{2,0,1:T(8,128)(2,1)} %bitcast.93), calls=%async_computation | async-start | bytes 262144 | tf_op jit(solution)/shard_map/all_to_all | solution.py:163
  139.6 1.3 copy-start.11
  139.6 1.3 copy-start.12
Sparse Core Ops, SparseCore 0:
  10.3 19.4 all-gather.3
  31.9 16.7 all-gather.5
where the time goes:
time: 150 us; the launch traced here: 149 us
  blocking collectives  55.4 us (37%)
  local copies, waits for them, and re-layouts  45.8 us (31%)
  matrix products  16.4 us (11%)
  between operations  14.5 us (10%)
  starting transfers between devices  10.4 us (7%)
  other arithmetic  5.47 us (4%)
    all_gather x1, blocking collectives, local(): bias_rows = lax.all_gather(bias_local, 'gx', axis=2, tiled=True)  16.1 us
    all_gather x1, blocking collectives, local(): lax.all_gather(left_side, 'gx', axis=0, tiled=True)  14.1 us
    all_gather x1, blocking collectives, local(): lax.all_gather(validity_mask, 'gx', axis=0, tiled=True)  13.5 us
    another operation x2, local copies, waits for them, and re-layouts  12.3 us
    transpose x2, local copies, waits for them, and re-layouts, outer_panel(): outer_block = outer_block.reshape(panel_rows, side_width, residue_total,...  11.8 us
    reshape x2, local copies, waits for them, and re-layouts, outer_panel(): outer_block.reshape(panel_rows, side_width, residue_total, side_width)  8.7 us
    all_gather x1, blocking collectives, local(): lax.all_gather(validity_mask, ('gy', 'gz'), axis=1, tiled=True)  6.22 us
    all_gather x1, blocking collectives, local(): lax.all_gather(right_side, ('gy', 'gz'), axis=1, tiled=True)  5.42 us
  transfers between devices with their start and end apart: 4, of which 0 were waited for; matrix products, arithmetic and copies ran while one was open for 9% of the time, Pallas kernels for 0%

commit v1 on v0

v1 whole, which is shorter than its diff:
```python
import functools

import jax
import jax.numpy as jnp
from jax import lax
from jax.experimental import pallas as pl
from jax.experimental.pallas import tpu as pltpu
from jax.sharding import PartitionSpec as P

MESH = pl.DeviceIdType.MESH
F32, BF16 = jnp.float32, jnp.bfloat16


def standardize(values):
    average = jnp.mean(values, axis=-1, keepdims=True)
    centred = values - average
    return centred * lax.rsqrt(jnp.mean(centred * centred, axis=-1, keepdims=True) + 1e-05)


def contract(a, b, dim_a, dim_b, precision=None):
    return lax.dot_general(
        a, b, (((dim_a,), (dim_b,)), ((), ())), precision=precision, preferred_element_type=F32
    )


def kernel(
    sizes,
    ids, hp, mask, pf, tab, wq, wk, wv, wg, wo, wb, w1, w2, wm, ww, wn,
    prof_out, pair_out,
    xg, idg, mg, mx, mc, bx, lg, zs, zr,
    ida, pen, bias, xown, qown, gown, lf, zf, lmask, wt, wf, rbd, osc,
    hy_s, hy_r, hz_s, hz_r, ig_s, ig_r, mg_s, mg_r, mx_s, mx_r, mc_s, mc_r,
    bx_s, bx_r, lg_s, lg_r, zr_s, zr_r, lc_s,
):
    nx, ny, nz, chunk = sizes
    nr = ny * nz
    seqs, res, depth = hp.shape
    heads = wb.shape[1]
    hd = depth // heads
    side = w1.shape[1]
    zdim = pf.shape[2]
    kinds = tab.shape[0]
    keys = nr * res
    pack = zdim // res
    grp = res // pack
    chunks = seqs // chunk
    q = lax.axis_index("gx")
    y = lax.axis_index("gy")
    z = lax.axis_index("gz")
    r = y * nz + z

    def at_r(index):
        return {"gy": index // nz, "gz": index % nz}

    barrier = pltpu.get_barrier_semaphore()
    for k in range(1, nr):
        pl.semaphore_signal(barrier, inc=1, device_id=at_r((r + k) % nr), device_id_type=MESH)
    for k in range(1, nx):
        pl.semaphore_signal(barrier, inc=1, device_id={"gx": (q + k) % nx}, device_id_type=MESH)
    for k in range(nx):
        @pl.when(jnp.logical_or(q != k, r != q))
        def _():
            pl.semaphore_signal(
                barrier, inc=1, device_id={"gx": k, **at_r(q)}, device_id_type=MESH
            )
    diagonal = jnp.where(q == r, 1, 0)
    pl.semaphore_wait(barrier, (nr - 1) + (nx - 1) + nr - diagonal)

    def remote(src, dst, send, recv, device):
        return pltpu.make_async_remote_copy(
            src_ref=src, dst_ref=dst, send_sem=send, recv_sem=recv,
            device_id=device, device_id_type=MESH,
        )

    def hy(k, c):
        part = pl.ds(c * chunk, chunk)
        return remote(
            hp.at[part], xg.at[r, part], hy_s.at[k - 1, c], hy_r.at[k - 1, c],
            {"gy": (y + k) % ny},
        )

    def hz(k, m, c):
        part = pl.ds(c * chunk, chunk)
        slot = ((y + ny - k) % ny) * nz + z
        src = hp.at[part] if k == 0 else xg.at[slot, part]
        return remote(
            src, xg.at[slot, part], hz_s.at[k, m - 1, c], hz_r.at[k, m - 1, c],
            {"gz": (z + m) % nz},
        )

    def ig(k):
        return remote(ids, idg.at[r], ig_s.at[k - 1], ig_r.at[k - 1], at_r((r + k) % nr))

    def mgc(k):
        return remote(mask, mg.at[r], mg_s.at[k - 1], mg_r.at[k - 1], at_r((r + k) % nr))

    def gxc(buffer, send, recv, k):
        return remote(
            buffer.at[q], buffer.at[q], send.at[k - 1], recv.at[k - 1], {"gx": (q + k) % nx}
        )

    def crossing(src, buffer, send, recv, k):
        return remote(src, buffer.at[q], send.at[k], recv.at[q], {"gx": r, **at_r(k)})

    def crossing_wait(src, buffer, send, recv, k):
        return remote(src, buffer.at[k], send.at[0], recv.at[k], {"gx": k, **at_r(q)})

    for c in range(chunks):
        for k in range(1, ny):
            hy(k, c).start()
    for k in range(1, nr):
        ig(k).start()
        mgc(k).start()
    for c in range(chunks):
        for m in range(1, nz):
            hz(0, m, c).start()
    own = pltpu.make_async_copy(hp, xg.at[r], lc_s)
    own.start()
    mx[q] = mask[...]
    for k in range(1, nx):
        remote(mask, mx.at[q], mx_s.at[k - 1], mx_r.at[k - 1], {"gx": (q + k) % nx}).start()
    for k in range(nr):
        @pl.when(jnp.logical_or(q != r, r != k))
        def _():
            crossing(mask, mc, mc_s, mc_r, k).start()

    @pl.when(q == r)
    def _():
        mc[q] = mask[...]

    pair_rows = pf[...].astype(F32).reshape(res * res, zdim)
    bx[q] = contract(wb[...], standardize(pair_rows), 0, 1, lax.Precision.HIGHEST)
    for k in range(1, nx):
        gxc(bx, bx_s, bx_r, k).start()

    label = lax.broadcasted_iota(jnp.int32, (kinds, res), 0)
    table = tab[...]
    for s in range(seqs):
        hot = jnp.where(label == ids[s : s + 1, :], 1.0, 0.0).astype(BF16)
        xown[s * res : (s + 1) * res, :] = hp[s].astype(F32) + contract(hot, table, 0, 0)
    normed = standardize(xown[...]).astype(BF16)
    qown[...] = jnp.dot(normed, wq[...], preferred_element_type=F32).astype(BF16)
    gown[...] = jax.nn.sigmoid(jnp.dot(normed, wg[...], preferred_element_type=F32))

    wf[...] = wm[...].astype(F32)
    for d in range(side):
        wt[:, d * side : (d + 1) * side] = wf[pl.ds(d, side, stride=side), :].T.astype(BF16)

    spread = jnp.where(
        lax.broadcasted_iota(jnp.int32, (grp, grp * side), 0)
        == lax.broadcasted_iota(jnp.int32, (grp, grp * side), 1) // side,
        1.0, 0.0,
    ).astype(BF16)
    maskf = mask[...].astype(F32)
    for p in range(pack):
        lmask[p * seqs : (p + 1) * seqs, :] = jnp.dot(
            maskf[:, p * grp : (p + 1) * grp].astype(BF16), spread, preferred_element_type=F32
        )
    mask4 = jnp.concatenate([maskf] * pack, axis=1)

    idg[r] = ids[...]
    mg[r] = mask[...]
    for k in range(1, nr):
        ig(k).wait_recv()
        mgc(k).wait_recv()
    ida[...] = jnp.concatenate([idg[k] for k in range(nr)], axis=1)
    pen[...] = (
        jnp.concatenate([mg[k] for k in range(nr)], axis=1).astype(F32) - 1.0
    ) * 1000000000.0

    for k in range(1, nx):
        remote(mask, mx.at[q], mx_s.at[k - 1], mx_r.at[k - 1], {"gx": (q + k) % nx}).wait_recv()
    for k in range(nx):
        @pl.when(jnp.logical_or(q != r, q != k))
        def _():
            crossing_wait(mask, mc, mc_s, mc_r, k).wait_recv()
    count = contract(
        mx[...].reshape(nx * seqs, res).astype(F32), mc[...].reshape(nx * seqs, res).astype(F32), 0, 0
    )
    share = 1.0 / (
        jnp.concatenate([count[p * grp : (p + 1) * grp, :] for p in range(pack)], axis=1) + 1.0
    )

    for k in range(1, nx):
        gxc(bx, bx_s, bx_r, k).wait_recv()
    for i in range(res):
        bias[:, i, :] = jnp.concatenate(
            [bx[k, :, i * res : (i + 1) * res] for k in range(nx)], axis=1
        )
    own.wait()

    scale = hd ** (-0.5)
    label_all = lax.broadcasted_iota(jnp.int32, (kinds, keys), 0)
    lane_head = lax.broadcasted_iota(jnp.int32, (res, depth), 1) // hd
    lane_block = lax.broadcasted_iota(jnp.int32, (seqs, zdim), 1) // res
    lane_block8 = lax.broadcasted_iota(jnp.int32, (side // pack, zdim), 1) // res
    w1x = jnp.concatenate([w1[...]] * pack, axis=1)

    def step(c, carry):
        for k in range(1, ny):
            hy(k, c).wait_recv()
            for m in range(1, nz):
                hz(k, m, c).start()
        for k in range(ny):
            for m in range(1, nz):
                hz(k, m, c).wait_recv()
        first = c * chunk
        normed_rows = []
        for t in range(chunk):
            hot = jnp.where(label_all == ida[pl.ds(first + t, 1), :], 1.0, 0.0).astype(BF16)
            rows = jnp.concatenate([xg[k, first + t] for k in range(nr)], axis=0).astype(F32)
            normed_rows.append(standardize(rows + contract(hot, table, 0, 0)).astype(BF16))
        normed_rows = jnp.concatenate(normed_rows, axis=0)
        key_rows = jnp.dot(normed_rows, wk[...], preferred_element_type=F32).astype(BF16)
        value_rows = jnp.dot(normed_rows, wv[...], preferred_element_type=F32).astype(BF16)
        bias_rows = bias[...].reshape(heads * res, keys)
        attended = []
        for t in range(chunk):
            base = pl.multiple_of((first + t) * res, res)
            query = qown[pl.ds(base, res), :]
            spread_query = jnp.concatenate(
                [jnp.where(lane_head == h, query, jnp.zeros_like(query)) for h in range(heads)],
                axis=0,
            )
            scores = contract(spread_query, key_rows[t * keys : (t + 1) * keys], 1, 1) * scale
            scores = scores + bias_rows + pen[pl.ds(first + t, 1), :]
            top = jnp.max(scores, axis=-1, keepdims=True)
            weights = jnp.exp(scores - top)
            total = jnp.sum(weights, axis=-1, keepdims=True)
            mixed = jnp.dot(
                weights.astype(BF16), value_rows[t * keys : (t + 1) * keys],
                preferred_element_type=F32,
            ) * (1.0 / total)
            picked = mixed[0:res]
            for h in range(1, heads):
                picked = jnp.where(lane_head == h, mixed[h * res : (h + 1) * res], picked)
            attended.append((gown[pl.ds(base, res), :] * picked).astype(BF16))
        base = pl.multiple_of(first * res, chunk * res)
        refreshed = (
            xown[pl.ds(base, chunk * res), :]
            + jnp.dot(jnp.concatenate(attended, axis=0), wo[...], preferred_element_type=F32)
        ).astype(BF16)
        prof_out[pl.ds(first, chunk)] = refreshed.reshape(chunk, res, depth)
        opm = standardize(refreshed.astype(F32)).astype(BF16)
        lf[pl.ds(base, chunk * res), :] = jnp.dot(opm, w1x, preferred_element_type=F32)
        right = contract(w2[...], opm, 0, 1)
        eighth = side // pack
        for t in range(chunk):
            tile = None
            for p in range(pack):
                shift = ((p - t) * res) % (chunk * res)
                piece = right[p * eighth : (p + 1) * eighth, :]
                piece = pltpu.roll(piece, shift, 1) if shift else piece
                tile = piece if tile is None else jnp.where(lane_block8 == p, piece, tile)
            zf[:, pl.ds(first + t, 1), :] = tile[:, None, :]
        return carry

    lax.fori_loop(0, chunks, step, 0)

    for p in range(pack):
        for half in range(grp // pack):
            tile = None
            for b in range(pack):
                piece = lf[pl.ds(p * grp + half * pack + b, seqs, stride=res), :]
                tile = piece if tile is None else jnp.where(lane_block == b, piece, tile)
            rows, lanes = slice(p * seqs, (p + 1) * seqs), slice(half * zdim, (half + 1) * zdim)
            lg[q, rows, lanes] = (tile * lmask[rows, lanes]).astype(BF16)
    for k in range(1, nx):
        gxc(lg, lg_s, lg_r, k).start()
    zs[...] = (zf[...] * mask4[None]).astype(BF16)
    for k in range(nr):
        @pl.when(jnp.logical_or(q != r, r != k))
        def _():
            crossing(zs, zr, zr_s, zr_r, k).start()

    @pl.when(q == r)
    def _():
        zr[q] = zs[...]

    eighth = side // pack
    place_row = lax.broadcasted_iota(jnp.int32, (zdim, pack * zdim), 0)
    place_col = lax.broadcasted_iota(jnp.int32, (zdim, pack * zdim), 1)
    placing = jnp.where(
        (place_row // res == place_col // zdim) & (place_row % res == place_col % res), 1.0, 0.0
    ).astype(BF16)
    for k in range(nx):
        @pl.when(jnp.logical_or(q != r, q != k))
        def _():
            crossing_wait(zs, zr, zr_s, zr_r, k).wait_recv()
    for k in range(nx):
        wide = jnp.dot(
            zr[k].reshape(eighth * seqs, zdim), placing, preferred_element_type=F32
        ).astype(BF16)
        for e in range(eighth):
            for p in range(pack):
                piece = wide[e * seqs : (e + 1) * seqs, p * zdim : (p + 1) * zdim]
                d = p * eighth + e
                for b in range(pack):
                    row = (k * pack + b) * seqs
                    rbd[row : row + seqs, d * zdim : (d + 1) * zdim] = jnp.where(
                        lane_block == b, piece, jnp.zeros_like(piece)
                    )
    for k in range(1, nx):
        gxc(lg, lg_s, lg_r, k).wait_recv()
    left = lg[...].reshape(nx * pack * seqs, grp * side)
    for e in range(eighth):
        cols = slice(e * pack * zdim, (e + 1) * pack * zdim)
        product = contract(left, rbd[:, cols], 0, 0).astype(BF16)
        for p in range(pack):
            d = e * pack + p
            for g in range(grp):
                osc[d * side : (d + 1) * side, g * zdim : (g + 1) * zdim] = product[
                    g * side : (g + 1) * side, p * zdim : (p + 1) * zdim
                ]
    for g in range(0, grp, 2):
        both = jnp.dot(
            wt[...], osc[:, g * zdim : (g + 2) * zdim], preferred_element_type=F32
        )
        middle = []
        for u in range(2):
            part = both[:, u * zdim : (u + 1) * zdim] * share[g + u : g + u + 1, :]
            pair_g = jnp.concatenate([pf[p * grp + g + u] for p in range(pack)], axis=0)
            middle.append(pair_g.astype(F32) + part.T)
        middle = jnp.concatenate(middle, axis=0)
        trans = standardize(middle).astype(BF16)
        expanded = jnp.maximum(
            jnp.dot(trans, ww[...], preferred_element_type=F32), 0.0
        ).astype(BF16)
        result = (middle + jnp.dot(expanded, wn[...], preferred_element_type=F32)).astype(BF16)
        for u in range(2):
            for p in range(pack):
                start = u * zdim + p * res
                pair_out[p * grp + g + u] = result[start : start + res]

    for c in range(chunks):
        for k in range(1, ny):
            hy(k, c).wait_send()
        for k in range(ny):
            for m in range(1, nz):
                hz(k, m, c).wait_send()
    for k in range(1, nr):
        ig(k).wait_send()
        mgc(k).wait_send()
    for k in range(1, nx):
        remote(mask, mx.at[q], mx_s.at[k - 1], mx_r.at[k - 1], {"gx": (q + k) % nx}).wait_send()
        gxc(bx, bx_s, bx_r, k).wait_send()
        gxc(lg, lg_s, lg_r, k).wait_send()
    for k in range(nr):
        @pl.when(jnp.logical_or(q != r, r != k))
        def _():
            crossing(mask, mc, mc_s, mc_r, k).wait_send()
            crossing(zs, zr, zr_s, zr_r, k).wait_send()


def solution(mesh):
    nx, ny, nz = mesh.shape["gx"], mesh.shape["gy"], mesh.shape["gz"]
    nr = ny * nz

    def local(*arrays):
        hp, pf, wb, w1, wm = arrays[1], arrays[3], arrays[10], arrays[11], arrays[13]
        seqs, res, depth = hp.shape
        zdim = pf.shape[2]
        heads, side = wb.shape[1], w1.shape[1]
        keys, pack = nr * res, zdim // res
        grp = res // pack
        chunk = pack
        chunks = seqs // chunk
        dma = pltpu.SemaphoreType.DMA
        vm = pltpu.VMEM
        scratch = [
            vm((nr, seqs, res, depth), BF16),
            vm((nr, seqs, res), jnp.int32),
            vm((nr, seqs, res), jnp.int32),
            vm((nx, seqs, res), jnp.int32),
            vm((nx, seqs, res), jnp.int32),
            vm((nx, heads, res * res), F32),
            vm((nx, pack * seqs, grp * side), BF16),
            vm((side // pack, seqs, zdim), BF16),
            vm((nx, side // pack, seqs, zdim), BF16),
            vm((seqs, keys), jnp.int32),
            vm((seqs, keys), F32),
            vm((heads, res, keys), F32),
            vm((seqs * res, depth), F32),
            vm((seqs * res, depth), BF16),
            vm((seqs * res, depth), F32),
            vm((seqs * res, zdim), F32),
            vm((side // pack, seqs, zdim), F32),
            vm((pack * seqs, grp * side), F32),
            vm((zdim, side * side), BF16),
            vm(wm.shape, F32),
            vm((nx * pack * seqs, side * zdim), BF16),
            vm((side * side, res * res), BF16),
            dma((max(ny - 1, 1), chunks)), dma((max(ny - 1, 1), chunks)),
            dma((ny, max(nz - 1, 1), chunks)), dma((ny, max(nz - 1, 1), chunks)),
            dma((nr,)), dma((nr,)), dma((nr,)), dma((nr,)),
            dma((nx,)), dma((nx,)), dma((nr,)), dma((nx,)),
            dma((nx,)), dma((nx,)), dma((nx,)), dma((nx,)),
            dma((nr,)), dma((nx,)), dma,
        ]
        return pl.pallas_call(
            functools.partial(kernel, (nx, ny, nz, chunk)),
            out_shape=(
                jax.ShapeDtypeStruct(hp.shape, BF16),
                jax.ShapeDtypeStruct(pf.shape, BF16),
            ),
            in_specs=[pl.BlockSpec(memory_space=pltpu.VMEM)] * len(arrays),
            out_specs=(pl.BlockSpec(memory_space=pltpu.VMEM),) * 2,
            scratch_shapes=scratch,
            compiler_params=pltpu.CompilerParams(
                collective_id=0, has_side_effects=True, vmem_limit_bytes=60 * 1024 * 1024
            ),
        )(*arrays)

    in_specs = (
        P(("grp", "gx"), ("gy", "gz")),
        P(("grp", "gx"), ("gy", "gz"), None),
        P(("grp", "gx"), ("gy", "gz")),
        P(("grp", "gy", "gz"), "gx", None),
    ) + (P(),) * 12
    out_specs = (P(("grp", "gx"), ("gy", "gz"), None), P(("grp", "gy", "gz"), "gx", None))
    return jax.shard_map(local, mesh=mesh, in_specs=in_specs, out_specs=out_specs, check_vma=False)
```

time: 150 us -> 48.6 us (0.32)
  blocking collectives: 55.4 us -> 0 us
  Pallas kernels: 0 us -> 41.8 us
  local copies, waits for them, and re-layouts: 45.8 us -> 5.3 us
  matrix products: 16.4 us -> 0 us
  between operations: 14.5 us -> 0.66 us
  starting transfers between devices: 10.4 us -> 0 us
  other arithmetic: 5.47 us -> 0 us
    all_gather x5 -> x0, blocking collectives: 55.4 us -> none  [the longest x1 16.1 us: local(): bias_rows = lax.all_gather(bias_local, 'gx', axis=2, tiled=True)]
    pallas_call x0 -> x1, Pallas kernels: none -> 41.8 us  [local(): pl.pallas_call(functools.partial(kernel, (nx, ny, nz, chunk)), out_shape=...]
    dot_general x17 -> x0, matrix products: 16.4 us -> none  [the longest x1 3.31 us: attend(): jnp.einsum('sihj,sjhd->sihd', exp_scores.astype(jnp.bfloat16), value_piec...]
    another operation x3 -> x0, local copies, waits for them, and re-layouts: 13.8 us -> none
    transpose x3 -> x0, local copies, waits for them, and re-layouts: 12 us -> none  [the longest x2 11.8 us: outer_panel(): outer_block = outer_block.reshape(panel_rows, side_width, residue_total,...]
    reshape x5 -> x0, local copies, waits for them, and re-layouts: 10.4 us -> none  [the longest x2 8.7 us: outer_panel(): outer_block.reshape(panel_rows, side_width, residue_total, side_width)]
    all_to_all x2 -> x0, starting transfers between devices: 10.4 us -> none  [the longest x1 5.32 us: local(): lax.all_to_all(mask_wide, 'gx', split_axis=1, concat_axis=0, tiled=True)]
    all_gather x4 -> x0, local copies, waits for them, and re-layouts: 4.74 us -> none  [the longest x1 2.27 us: local(): lax.all_gather(values_local, ('gy', 'gz'), axis=1, tiled=True)]
  transfers between devices with their start and end apart: 4 -> 0, of which waited for: 0 -> 0; matrix products, arithmetic and copies ran while one was open for 9% -> 0% of each run, Pallas kernels for 0% -> 0%
where the time goes in v1:
time: 48.6 us; the launch traced here: 47.8 us
  Pallas kernels  41.8 us (86%)
  local copies, waits for them, and re-layouts  5.3 us (11%)
  between operations  0.66 us (1%)
    pallas_call x1, Pallas kernels, local(): pl.pallas_call(functools.partial(kernel, (nx, ny, nz, chunk)), out_shape=...  41.8 us
    unnamed x11, local copies, waits for them, and re-layouts  5.3 us

profile of v1, /device:TPU:0, one launch (start us, length us, event | category | flops | bytes accessed | tf_op | source)
XLA Modules:
  0.0 47.8 jit_solution(1698861327169337501)
XLA Ops:
  0.6 0.0 copy-start.1
  0.6 1.4 %copy.18.wb = f32[128,8]{1,0:T(8,128)} copy(f32[128,8]{0,1:T(8,128)} %param.26) | data formatting | bytes 8192 | tf_op args[10]
  2.1 0.0 copy-done.1
  2.1 0.0 copy-start.2
  2.1 0.7 %copy.19.w1 = bf16[256,32]{1,0:T(8,128)(2,1)} copy(bf16[256,32]{0,1:T(8,128)(2,1)S(1)} %copy-done.1) | data formatting | bytes 32768 | tf_op args[11]
  2.8 0.0 copy-done.2
  2.8 0.7 %copy.20.w2 = bf16[256,32]{1,0:T(8,128)(2,1)} copy(bf16[256,32]{0,1:T(8,128)(2,1)S(1)} %copy-done.2) | data formatting | bytes 32768 | tf_op args[12]
  3.5 41.8 %shard_map.167 = (bf16[16,32,256]{2,1,0:T(8,128)(2,1)}, bf16[32,32,128]{2,1,0:T(8,128)(2,1)}) custom-call(s32[16,32]{1,0:T(8,128)} %ids.1, bf16[16,32,256]{2,1,0:T(8,128)(2,1)} %hp.1, s32[16,32]{1,0:T(8,128)} %mask.1, bf16[32,32,128]{2,1,0:T(8,128)(2,1)} %pf.1, bf16[23,256]{1,0:T(8,128)(2,1)} %tab.1, bf16[256,256]{1,0:T(8,128)(2,1)} %wq.1, ...), custom_call_target="tpu_custom_call" | custom-call | tf_op jit(solution)/shard_map/pallas_call | solution.py:400
  45.3 0.0 copy-start
  45.3 1.7 %copy.23 = bf16[16,32,256]{2,1,0:T(8,128)(2,1)} copy(bf16[16,32,256]{2,1,0:T(8,128)(2,1)} %get-tuple-element.4) | data formatting | bytes 524288
  47.1 0.0 copy-done
  47.1 0.7 %copy.24 = bf16[32,32,128]{2,1,0:T(8,128)(2,1)} copy(bf16[32,32,128]{2,1,0:T(8,128)(2,1)S(1)} %copy-done) | data formatting | bytes 524288
Async XLA Ops:
  0.6 1.4 %copy-start.1 = (bf16[256,32]{0,1:T(8,128)(2,1)S(1)}, bf16[256,32]{0,1:T(8,128)(2,1)}, u32[]{:S(2)}) copy-start(bf16[256,32]{0,1:T(8,128)(2,1)} %param.27) | copy-start | bytes 49156
  2.1 0.7 %copy-start.2 = (bf16[256,32]{0,1:T(8,128)(2,1)S(1)}, bf16[256,32]{0,1:T(8,128)(2,1)}, u32[]{:S(2)}) copy-start(bf16[256,32]{0,1:T(8,128)(2,1)} %param.28) | copy-start | bytes 49156
  45.3 1.7 %copy-start = (bf16[32,32,128]{2,1,0:T(8,128)(2,1)S(1)}, bf16[32,32,128]{2,1,0:T(8,128)(2,1)}, u32[]{:S(2)}) copy-start(bf16[32,32,128]{2,1,0:T(8,128)(2,1)} %get-tuple-element.5) | copy-start | bytes 786436

commit v2 on v1

--- a/solution.py
+++ b/solution.py
@@ -8,6 +8,7 @@
 from jax.sharding import PartitionSpec as P
 
 MESH = pl.DeviceIdType.MESH
+LATE = (3, 5, 6, 7, 8, 9, 13, 14, 15)
 F32, BF16 = jnp.float32, jnp.bfloat16
 
 
@@ -25,19 +26,24 @@
 
 def kernel(
     sizes,
-    ids, hp, mask, pf, tab, wq, wk, wv, wg, wo, wb, w1, w2, wm, ww, wn,
+    ids, hp, mask, hf, tab, hq, hk, hv, hg, ho, wb, w1, w2, hm, hw, hn,
     prof_out, pair_out,
     xg, idg, mg, mx, mc, bx, lg, zs, zr,
     ida, pen, bias, xown, qown, gown, lf, zf, lmask, wt, wf, rbd, osc,
     hy_s, hy_r, hz_s, hz_r, ig_s, ig_r, mg_s, mg_r, mx_s, mx_r, mc_s, mc_r,
-    bx_s, bx_r, lg_s, lg_r, zr_s, zr_r, lc_s,
+    bx_s, bx_r, lg_s, lg_r, zr_s, zr_r, lc_s, sw_s, sw_r,
+    vf, vq, vk, vv, vg, vo, vm_, vw, vn, load_s,
 ):
     nx, ny, nz, chunk = sizes
+    pf, wq, wk, wv, wg, wo, wm, ww, wn = vf, vq, vk, vv, vg, vo, vm_, vw, vn
+    far = (hf, hq, hk, hv, hg, ho, hm, hw, hn)
+    near = (pf, wq, wk, wv, wg, wo, wm, ww, wn)
+    loads = [pltpu.make_async_copy(a, b, load_s.at[k]) for k, (a, b) in enumerate(zip(far, near))]
     nr = ny * nz
     seqs, res, depth = hp.shape
-    heads = wb.shape[1]
+    heads = wb.shape[0]
     hd = depth // heads
-    side = w1.shape[1]
+    side = w1.shape[0]
     zdim = pf.shape[2]
     kinds = tab.shape[0]
     keys = nr * res
@@ -63,6 +69,8 @@
             pl.semaphore_signal(
                 barrier, inc=1, device_id={"gx": k, **at_r(q)}, device_id_type=MESH
             )
+    for load in loads:
+        load.start()
     diagonal = jnp.where(q == r, 1, 0)
     pl.semaphore_wait(barrier, (nr - 1) + (nx - 1) + nr - diagonal)
 
@@ -102,34 +110,47 @@
     def crossing(src, buffer, send, recv, k):
         return remote(src, buffer.at[q], send.at[k], recv.at[q], {"gx": r, **at_r(k)})
 
+    def swap():
+        return remote(zs, zr.at[q], sw_s, sw_r, {"gx": r, **at_r(q)})
+
+    def swap_wait():
+        return remote(zs, zr.at[r], sw_s, sw_r, {"gx": r, **at_r(q)})
+
+    def spread_right(k):
+        return remote(
+            zr.at[r], zr.at[r], zr_s.at[k - 1], zr_r.at[k - 1], at_r((r + k) % nr)
+        )
+
     def crossing_wait(src, buffer, send, recv, k):
         return remote(src, buffer.at[k], send.at[0], recv.at[k], {"gx": k, **at_r(q)})
+
+    for k in range(1, nr):
+        ig(k).start()
+        mgc(k).start()
+    mx[q] = mask[...]
+    for k in range(1, nx):
+        remote(mask, mx.at[q], mx_s.at[k - 1], mx_r.at[k - 1], {"gx": (q + k) % nx}).start()
+    for k in range(nr):
+        @pl.when(jnp.logical_or(q != r, r != k))
+        def _():
+            crossing(mask, mc, mc_s, mc_r, k).start()
+
+    @pl.when(q == r)
+    def _():
+        mc[q] = mask[...]
 
     for c in range(chunks):
         for k in range(1, ny):
             hy(k, c).start()
-    for k in range(1, nr):
-        ig(k).start()
-        mgc(k).start()
     for c in range(chunks):
         for m in range(1, nz):
             hz(0, m, c).start()
     own = pltpu.make_async_copy(hp, xg.at[r], lc_s)
     own.start()
-    mx[q] = mask[...]
-    for k in range(1, nx):
-        remote(mask, mx.at[q], mx_s.at[k - 1], mx_r.at[k - 1], {"gx": (q + k) % nx}).start()
-    for k in range(nr):
-        @pl.when(jnp.logical_or(q != r, r != k))
-        def _():
-            crossing(mask, mc, mc_s, mc_r, k).start()
-
-    @pl.when(q == r)
-    def _():
-        mc[q] = mask[...]
-
+
+    loads[0].wait()
     pair_rows = pf[...].astype(F32).reshape(res * res, zdim)
-    bx[q] = contract(wb[...], standardize(pair_rows), 0, 1, lax.Precision.HIGHEST)
+    bx[q] = contract(wb[...], standardize(pair_rows), 1, 1, lax.Precision.HIGHEST)
     for k in range(1, nx):
         gxc(bx, bx_s, bx_r, k).start()
 
@@ -139,6 +160,8 @@
         hot = jnp.where(label == ids[s : s + 1, :], 1.0, 0.0).astype(BF16)
         xown[s * res : (s + 1) * res, :] = hp[s].astype(F32) + contract(hot, table, 0, 0)
     normed = standardize(xown[...]).astype(BF16)
+    for load in loads[1:]:
+        load.wait()
     qown[...] = jnp.dot(normed, wq[...], preferred_element_type=F32).astype(BF16)
     gown[...] = jax.nn.sigmoid(jnp.dot(normed, wg[...], preferred_element_type=F32))
 
@@ -194,13 +217,17 @@
     lane_head = lax.broadcasted_iota(jnp.int32, (res, depth), 1) // hd
     lane_block = lax.broadcasted_iota(jnp.int32, (seqs, zdim), 1) // res
     lane_block8 = lax.broadcasted_iota(jnp.int32, (side // pack, zdim), 1) // res
-    w1x = jnp.concatenate([w1[...]] * pack, axis=1)
-
-    def step(c, carry):
+    w1x = jnp.concatenate([w1[...]] * pack, axis=0)
+
+    def pass_on(c):
         for k in range(1, ny):
             hy(k, c).wait_recv()
             for m in range(1, nz):
                 hz(k, m, c).start()
+
+    pass_on(0)
+
+    def step(c, carry):
         for k in range(ny):
             for m in range(1, nz):
                 hz(k, m, c).wait_recv()
@@ -235,6 +262,10 @@
             for h in range(1, heads):
                 picked = jnp.where(lane_head == h, mixed[h * res : (h + 1) * res], picked)
             attended.append((gown[pl.ds(base, res), :] * picked).astype(BF16))
+        @pl.when(c + 1 < chunks)
+        def _():
+            pass_on(c + 1)
+
         base = pl.multiple_of(first * res, chunk * res)
         refreshed = (
             xown[pl.ds(base, chunk * res), :]
@@ -242,8 +273,8 @@
         ).astype(BF16)
         prof_out[pl.ds(first, chunk)] = refreshed.reshape(chunk, res, depth)
         opm = standardize(refreshed.astype(F32)).astype(BF16)
-        lf[pl.ds(base, chunk * res), :] = jnp.dot(opm, w1x, preferred_element_type=F32)
-        right = contract(w2[...], opm, 0, 1)
+        lf[pl.ds(base, chunk * res), :] = contract(opm, w1x, 1, 1)
+        right = contract(w2[...], opm, 1, 1)
         eighth = side // pack
         for t in range(chunk):
             tile = None
@@ -257,6 +288,11 @@
 
     lax.fori_loop(0, chunks, step, 0)
 
+    zs[...] = (zf[...] * mask4[None]).astype(BF16)
+    @pl.when(q != r)
+    def _():
+        swap().start()
+
     for p in range(pack):
         for half in range(grp // pack):
             tile = None
@@ -267,15 +303,16 @@
             lg[q, rows, lanes] = (tile * lmask[rows, lanes]).astype(BF16)
     for k in range(1, nx):
         gxc(lg, lg_s, lg_r, k).start()
-    zs[...] = (zf[...] * mask4[None]).astype(BF16)
-    for k in range(nr):
-        @pl.when(jnp.logical_or(q != r, r != k))
-        def _():
-            crossing(zs, zr, zr_s, zr_r, k).start()
-
     @pl.when(q == r)
     def _():
         zr[q] = zs[...]
+
+    @pl.when(q != r)
+    def _():
+        swap_wait().wait_recv()
+
+    for k in range(1, nr):
+        spread_right(k).start()
 
     eighth = side // pack
     place_row = lax.broadcasted_iota(jnp.int32, (zdim, pack * zdim), 0)
@@ -283,10 +320,8 @@
     placing = jnp.where(
         (place_row // res == place_col // zdim) & (place_row % res == place_col % res), 1.0, 0.0
     ).astype(BF16)
-    for k in range(nx):
-        @pl.when(jnp.logical_or(q != r, q != k))
-        def _():
-            crossing_wait(zs, zr, zr_s, zr_r, k).wait_recv()
+    for k in range(1, nr):
+        spread_right(k).wait_recv()
     for k in range(nx):
         wide = jnp.dot(
             zr[k].reshape(eighth * seqs, zdim), placing, preferred_element_type=F32
@@ -345,11 +380,17 @@
         remote(mask, mx.at[q], mx_s.at[k - 1], mx_r.at[k - 1], {"gx": (q + k) % nx}).wait_send()
         gxc(bx, bx_s, bx_r, k).wait_send()
         gxc(lg, lg_s, lg_r, k).wait_send()
+    for k in range(1, nr):
+        spread_right(k).wait_send()
+
+    @pl.when(q != r)
+    def _():
+        swap().wait_send()
+
     for k in range(nr):
         @pl.when(jnp.logical_or(q != r, r != k))
         def _():
             crossing(mask, mc, mc_s, mc_r, k).wait_send()
-            crossing(zs, zr, zr_s, zr_r, k).wait_send()
 
 
 def solution(mesh):
@@ -357,10 +398,13 @@
     nr = ny * nz
 
     def local(*arrays):
+        arrays = list(arrays)
+        for index in (10, 11, 12):
+            arrays[index] = arrays[index].T
         hp, pf, wb, w1, wm = arrays[1], arrays[3], arrays[10], arrays[11], arrays[13]
         seqs, res, depth = hp.shape
         zdim = pf.shape[2]
-        heads, side = wb.shape[1], w1.shape[1]
+        heads, side = wb.shape[0], w1.shape[0]
         keys, pack = nr * res, zdim // res
         grp = res // pack
         chunk = pack
@@ -395,15 +439,18 @@
             dma((nr,)), dma((nr,)), dma((nr,)), dma((nr,)),
             dma((nx,)), dma((nx,)), dma((nr,)), dma((nx,)),
             dma((nx,)), dma((nx,)), dma((nx,)), dma((nx,)),
-            dma((nr,)), dma((nx,)), dma,
-        ]
+            dma((nr,)), dma((nr,)), dma, dma, dma,
+        ] + [vm(arrays[k].shape, BF16) for k in LATE] + [dma((len(LATE),))]
         return pl.pallas_call(
             functools.partial(kernel, (nx, ny, nz, chunk)),
             out_shape=(
                 jax.ShapeDtypeStruct(hp.shape, BF16),
                 jax.ShapeDtypeStruct(pf.shape, BF16),
             ),
-            in_specs=[pl.BlockSpec(memory_space=pltpu.VMEM)] * len(arrays),
+            in_specs=[
+                pl.BlockSpec(memory_space=pl.ANY if k in LATE else pltpu.VMEM)
+                for k in range(len(arrays))
+            ],
             out_specs=(pl.BlockSpec(memory_space=pltpu.VMEM),) * 2,
             scratch_shapes=scratch,
             compiler_params=pltpu.CompilerParams(

time: 48.6 us -> 39 us (0.80); the launches traced: 47.8 us -> 38.8 us
  Pallas kernels: 41.8 us -> 35.7 us
  local copies, waits for them, and re-layouts: 5.3 us -> 2.42 us
    pallas_call x1, Pallas kernels: 41.8 us -> 35.7 us  [local(): pl.pallas_call(functools.partial(kernel, (nx, ny, nz, chunk)), out_shape=...]
    unnamed x11 -> x4, local copies, waits for them, and re-layouts: 5.3 us -> 2.42 us
where the time goes in v2:
time: 39 us; the launch traced here: 38.8 us
  Pallas kernels  35.7 us (92%)
  local copies, waits for them, and re-layouts  2.42 us (6%)
  between operations  0.65 us (2%)
    pallas_call x1, Pallas kernels, local(): pl.pallas_call(functools.partial(kernel, (nx, ny, nz, chunk)), out_shape=...  35.7 us
    unnamed x4, local copies, waits for them, and re-layouts  2.42 us

profile of v2, /device:TPU:0, one launch (start us, length us, event | category | flops | bytes accessed | tf_op | source)
XLA Modules:
  0.0 38.8 jit_solution(8770122976906204209)
XLA Ops:
  0.6 35.7 %shard_map.167 = (bf16[16,32,256]{2,1,0:T(8,128)(2,1)}, bf16[32,32,128]{2,1,0:T(8,128)(2,1)}) custom-call(s32[16,32]{1,0:T(8,128)} %ids.1, bf16[16,32,256]{2,1,0:T(8,128)(2,1)} %hp.1, s32[16,32]{1,0:T(8,128)} %mask.1, bf16[32,32,128]{2,1,0:T(8,128)(2,1)} %hf.1, bf16[23,256]{1,0:T(8,128)(2,1)} %tab.1, bf16[256,256]{1,0:T(8,128)(2,1)} %hq.1, ...), custom_call_target="tpu_custom_call" | custom-call | tf_op jit(solution)/shard_map/pallas_call | solution.py:444
  36.4 0.0 copy-start
  36.4 1.7 %copy.20 = bf16[16,32,256]{2,1,0:T(8,128)(2,1)} copy(bf16[16,32,256]{2,1,0:T(8,128)(2,1)} %get-tuple-element.4) | data formatting | bytes 524288
  38.1 0.0 copy-done
  38.1 0.7 %copy.21 = bf16[32,32,128]{2,1,0:T(8,128)(2,1)} copy(bf16[32,32,128]{2,1,0:T(8,128)(2,1)S(1)} %copy-done) | data formatting | bytes 524288
Async XLA Ops:
  36.4 1.7 %copy-start = (bf16[32,32,128]{2,1,0:T(8,128)(2,1)S(1)}, bf16[32,32,128]{2,1,0:T(8,128)(2,1)}, u32[]{:S(2)}) copy-start(bf16[32,32,128]{2,1,0:T(8,128)(2,1)} %get-tuple-element.5) | copy-start | bytes 786436
